TPU v7x, 32 devices: a whole 2x2x4 slice. The times are simulated.
32 devices in a mesh: groups: 2 (over x), docs: 16 (over z, y, core).
Axes of the slice: x: 2, y: 2, z: 4, core: 2. Of those that a mesh axis runs over, the one named last changes fastest.
Arguments:
- sentences: bfloat16 [65536, 1280], P(('groups', 'docs')), parts along dimension 0, may hold values from -10 to 10
- sent_doc: int32 [65536], P('groups'), parts along dimension 0, may hold values from 0 to 2047, never falling along the last dimension, each value on 1 to 32 neighbouring positions
- images: bfloat16 [8192, 1280], P(('groups', 'docs')), parts along dimension 0, may hold values from -30 to 30
- image_owner: int32 [8192, 1], P(('groups', 'docs')), parts along dimension 0, may hold values from 0 to 15, as said below
- anchor: int32 [8192], P(('groups', 'docs')), parts along dimension 0, may hold values from 0 to 2047, as said below
- loader_shard: int32 [8192, 1], P(('groups', 'docs')), parts along dimension 0, may hold values from 0 to 15, as said below
Outputs:
- loaded_images: bfloat16 [16384, 1280], P(('groups', 'docs')), parts along dimension 0
- loaded_text: bfloat16 [16384, 1280], P(('groups', 'docs')), parts along dimension 0
There are 2 independent parts, one for each index of `groups`. A program takes and returns all parts, laid end to end along the dimension named above; each array names one. Nothing has to cross between parts.
Inputs may be any that keep to these rules, and one draw needn't show every extreme that they name: `sent_doc`: documents are runs of 1 to 32 consecutive sentences, ids never falling. `image_owner`: the 256 images of one device name one owner at most 32 times, and some owner exactly 32 times. loader_shard = (a[source device] + b[image_owner]) mod 16 for two permutations a and b of the devices, drawn with the data. So the images of one device name one shard at most 32 times (some exactly 32), and the images that one owner receives from all devices name one shard at most 32 times, all from one source device. `anchor`: the image's document is the document of this sentence of its owner.
All inputs are finite; a program needn't handle non-finite values.
Results may differ from a plain program's by a relative error of at most 0.0048.
Values may be sent and summed in bfloat16 or wider, within the bound.
A program may use at most 64 MiB of HBM per device.

v0:
```python
import functools

import jax
import jax.numpy as jnp
from jax import lax
from jax.experimental import pallas as pl
from jax.experimental.pallas import tpu as pltpu
from jax.sharding import PartitionSpec as P

MOST_SENT = 32
LANES = 128
SUB = 8
MESH = pl.DeviceIdType.MESH
HIGH = lax.Precision.HIGHEST
TRANS_LHS = (((0,), (0,)), ((), ()))
TRANS_RHS = (((1,), (1,)), ((), ()))


def iota(shape, dim):
    return lax.broadcasted_iota(jnp.int32, shape, dim)


def ranks(keys, n):
    count = keys.shape[1]
    onehot = (keys == iota((n, count), 0)).astype(jnp.float32)
    above = (iota((count, count), 0) < iota((count, count), 1)).astype(jnp.bfloat16)
    counts = jnp.dot(onehot.astype(jnp.bfloat16), above, preferred_element_type=jnp.float32)
    return jnp.sum(counts * onehot, axis=0, keepdims=True).astype(jnp.int32)


def exchange_kernel(
    n, cap, block, tile, owner_ref, anchor_ref, shard_ref, images_ref, ids_ref, sent_ref,
    img_out, txt_out, meta_out,
    ext, far_images, far_owner_ref, far_shard_ref, disp, shrd, far_disp, far_shrd, arrived, aligned, tsend, meta_s, target_ref,
    local_sem, halo_send, halo_recv, raw_send, raw_recv, send_sem, recv_sem,
):
    me = lax.axis_index("docs")
    half = n // 2
    first = lax.div(me, half) * half
    across = lax.rem(first + half, n)
    partner = lax.rem(me + half, n)
    own_rows, feature = sent_ref.shape
    width = ext.shape[0]
    count = images_ref.shape[0]
    rows = n * block
    part = half * block
    temper = feature ** (-0.5)

    barrier = pltpu.get_barrier_semaphore()

    @pl.loop(1, n)
    def _(k):
        pl.semaphore_signal(barrier, inc=1, device_id={"docs": lax.rem(me + k, n)}, device_id_type=MESH)

    load = pltpu.make_async_copy(sent_ref, ext.at[pl.ds(MOST_SENT, own_rows)], local_sem.at[0])
    load.start()
    pl.semaphore_wait(barrier, n - 1)

    def raw(which):
        src, dst = ((owner_ref, far_owner_ref), (shard_ref, far_shard_ref), (images_ref, far_images))[which]
        return pltpu.make_async_remote_copy(
            src_ref=src, dst_ref=dst, send_sem=raw_send.at[which], recv_sem=raw_recv.at[which],
            device_id={"docs": partner}, device_id_type=MESH,
        )

    def halo(way):
        to = lax.rem(me + 1, n) if way == 0 else lax.rem(me + n - 1, n)
        src = own_rows - MOST_SENT if way == 0 else 0
        dst = 0 if way == 0 else own_rows + MOST_SENT
        return pltpu.make_async_remote_copy(
            src_ref=sent_ref.at[pl.ds(src, MOST_SENT)], dst_ref=ext.at[pl.ds(dst, MOST_SENT)],
            send_sem=halo_send.at[way], recv_sem=halo_recv.at[way],
            device_id={"docs": to}, device_id_type=MESH,
        )

    halo(0).start()
    halo(1).start()
    for which in range(3):
        raw(which).start()

    owner, anchor, shard = owner_ref[...], anchor_ref[...], shard_ref[...]
    rank = ranks(owner, n)
    lane = iota((LANES, count), 0)
    lead = rank == 0
    for_owner = jnp.where(lane == rank, anchor + 1, 0) + jnp.where((lane == cap) & lead, shard + 1, 0)
    for_shard = jnp.where((lane == cap + 1) & lead, owner + 1, 0)
    keyed = iota((n * SUB, count), 0)
    meta = lax.dot_general(
        (keyed == owner * SUB).astype(jnp.float32), for_owner.astype(jnp.float32), TRANS_RHS,
        precision=HIGH, preferred_element_type=jnp.float32,
    ) + lax.dot_general(
        (keyed == shard * SUB).astype(jnp.float32), for_shard.astype(jnp.float32), TRANS_RHS,
        precision=HIGH, preferred_element_type=jnp.float32,
    )
    meta_s[...] = meta.astype(jnp.int32)

    def fill(ref, key, order, values):
        place = key * block + order

        @pl.loop(0, part // tile)
        def _(t):
            base = pl.multiple_of(t * tile, tile)
            table = (place == iota((tile, count), 0) + (base + first * block)).astype(jnp.bfloat16)
            ref[pl.ds(base, tile), :] = jnp.dot(
                table, values[...], preferred_element_type=jnp.float32
            ).astype(jnp.bfloat16)

    fill(disp, owner, rank, images_ref)
    fill(shrd, shard, rank, images_ref)

    def at(ref, who, size):
        return ref.at[pl.ds(pl.multiple_of(who * size, size), size)]

    flows = (
        (meta_s, meta_out, SUB, True, False),
        (disp, arrived, block, False, False),
        (shrd, img_out, block, False, False),
        (tsend, txt_out, block, True, False),
        (far_disp, arrived, block, False, True),
        (far_shrd, img_out, block, False, True),
    )

    def remote(kind, peer, sender):
        src, dst, size, everyone, far = flows[kind]
        piece = peer if everyone else lax.rem(peer, half)
        slot = lax.rem(sender + half, n) if far else sender
        return pltpu.make_async_remote_copy(
            src_ref=at(src, piece, size), dst_ref=at(dst, slot, size),
            send_sem=send_sem.at[kind, peer], recv_sem=recv_sem.at[kind, sender],
            device_id={"docs": peer}, device_id_type=MESH,
        )

    def local(kind):
        src, dst, size, everyone, far = flows[kind]
        piece = me if everyone else me - first
        slot = partner if far else me
        return pltpu.make_async_copy(at(src, piece, size), at(dst, slot, size), local_sem.at[1 + kind])

    def each(kind, act):
        if flows[kind][3]:

            @pl.loop(0, half)
            def _(k):
                act(across + lax.rem(me - first + k, half))

        @pl.loop(1, half)
        def _(k):
            act(first + lax.rem(me - first + k, half))

    def start(kind):
        each(kind, lambda peer: remote(kind, peer, me).start())
        local(kind).start()

    def sent(kind):
        each(kind, lambda peer: remote(kind, peer, me).wait_send())

    def landed(kind):
        each(kind, lambda peer: remote(kind, peer, peer).wait_recv())
        local(kind).wait()

    start(0)
    start(1)
    start(2)
    load.wait()
    for way in (0, 1):
        halo(way).wait_recv()
    landed(0)
    ids = ids_ref[...]
    records = meta_out[...].astype(jnp.float32)

    def align(head):
        @pl.loop(0, part // tile)
        def _(t):
            base = pl.multiple_of(head * block + t * tile, tile)
            spot = iota((tile, n * SUB), 0) + base
            picker = (lax.div(spot, block) * SUB == iota((tile, n * SUB), 1)).astype(jnp.float32)
            picked = jnp.dot(picker, records, precision=HIGH, preferred_element_type=jnp.float32)
            picked = picked.astype(jnp.int32)
            step = lax.rem(iota((tile, 1), 0) + base, block)
            lanes = iota((tile, LANES), 1)
            anchored = jnp.sum(jnp.where((lanes == step) & (lanes < cap), picked, 0), axis=1, keepdims=True)
            goal = jnp.sum(jnp.where(lanes == cap, picked, 0), axis=1, keepdims=True)
            target_ref[pl.ds(base, tile), :] = (goal - 1) * block + step
            filled = anchored > 0
            here = iota((tile, width), 1) == anchored - 1 + MOST_SENT
            doc = jnp.sum(jnp.where(here, ids, 0), axis=1, keepdims=True)
            doc = jnp.where(filled, doc, -2)
            scores = lax.dot_general(
                arrived[pl.ds(base, tile), :], ext[...], TRANS_RHS, preferred_element_type=jnp.float32
            ) * temper
            member = doc == ids
            peak = jnp.max(jnp.where(member, scores, -1e30), axis=1, keepdims=True)
            raised = jnp.where(member, jnp.exp(scores - peak), 0.0)
            total = jnp.sum(raised, axis=1, keepdims=True)
            weights = (raised / jnp.where(filled, total, 1.0)).astype(jnp.bfloat16)
            aligned[pl.ds(base, tile), :] = jnp.dot(
                weights, ext[...], preferred_element_type=jnp.float32
            ).astype(jnp.bfloat16)

    def route(head, more):
        begin = pl.multiple_of(head * block, part)

        @pl.loop(0, rows // tile)
        def _(t):
            base = pl.multiple_of(t * tile, tile)
            table = target_ref[pl.ds(begin, part), :] == iota((part, tile), 1) + base
            moved = lax.dot_general(
                table.astype(jnp.bfloat16), aligned[pl.ds(begin, part), :], TRANS_LHS,
                preferred_element_type=jnp.float32,
            ).astype(jnp.bfloat16)
            if more:
                moved = tsend[pl.ds(base, tile), :] + moved
            tsend[pl.ds(base, tile), :] = moved

    landed(1)
    align(first)
    route(first, False)
    raw(0).wait_recv()
    raw(1).wait_recv()
    far_owner, far_shard = far_owner_ref[...], far_shard_ref[...]
    far_rank = ranks(far_owner, n)
    raw(2).wait_recv()
    fill(far_disp, far_owner, far_rank, far_images)
    start(4)
    fill(far_shrd, far_shard, far_rank, far_images)
    sent(4)
    landed(4)
    start(5)
    align(across)
    route(across, True)
    start(3)
    for way in (0, 1):
        halo(way).wait_send()
    for which in range(3):
        raw(which).wait_send()
    for kind in (0, 1, 2, 5):
        sent(kind)
    landed(2)
    landed(5)
    sent(3)
    landed(3)


def place_kernel(n, block, lane, meta_ref, img_ref, txt_ref, img_out, txt_out, buf, sems):
    copy = pltpu.make_async_copy(img_ref, img_out, sems.at[0])
    copy.start()
    for s in range(n):
        source = meta_ref[s * SUB, lane]
        rows = txt_ref[pl.ds(pl.multiple_of(jnp.maximum(source - 1, 0) * block, block), block), :]
        buf[pl.ds(s * block, block), :] = jnp.where(source > 0, rows, jnp.zeros_like(rows))
        pltpu.make_async_copy(
            buf.at[pl.ds(s * block, block)], txt_out.at[pl.ds(s * block, block)], sems.at[1 + s]
        ).start()
    for s in range(n):
        pltpu.make_async_copy(
            buf.at[pl.ds(s * block, block)], txt_out.at[pl.ds(s * block, block)], sems.at[1 + s]
        ).wait()
    copy.wait()


def shards(sentences, sent_doc, images, image_owner, anchor, loader_shard):
    n = lax.axis_size("docs")
    me = lax.axis_index("docs")
    own_rows, feature = sentences.shape
    count = images.shape[0]
    cap = max(4, 2 * count // n)
    block = -(-cap // 16) * 16
    rows = n * block
    tile = min(256, rows // 2)
    width = own_rows + 2 * MOST_SENT
    padded_ids = jnp.pad(sent_doc, (MOST_SENT, MOST_SENT), constant_values=-1)
    ids = lax.dynamic_slice_in_dim(padded_ids, me * own_rows, width)[None, :]
    half = jax.ShapeDtypeStruct((rows, feature), jnp.bfloat16)
    slots = pltpu.VMEM((rows, feature), jnp.bfloat16)
    some = pltpu.VMEM((rows // 2, feature), jnp.bfloat16)
    anywhere = pl.BlockSpec(memory_space=pl.ANY)
    dma = pltpu.SemaphoreType.DMA
    vmem = pl.BlockSpec(memory_space=pltpu.VMEM)
    got_img, got_txt, meta = pl.pallas_call(
        functools.partial(exchange_kernel, n, cap, block, tile),
        out_shape=(half, half, jax.ShapeDtypeStruct((n * SUB, LANES), jnp.int32)),
        in_specs=[vmem] * 5 + [anywhere],
        out_specs=(anywhere, anywhere, vmem),
        scratch_shapes=[
            pltpu.VMEM((width, feature), jnp.bfloat16),
            pltpu.VMEM((count, feature), jnp.bfloat16),
            pltpu.VMEM((1, count), jnp.int32),
            pltpu.VMEM((1, count), jnp.int32),
            some, some, some, some, slots, slots, slots,
            pltpu.VMEM((n * SUB, LANES), jnp.int32),
            pltpu.VMEM((rows, 1), jnp.int32),
            dma((7,)), dma((2,)), dma((2,)), dma((3,)), dma((3,)), dma((6, n)), dma((6, n)),
        ],
        compiler_params=pltpu.CompilerParams(
            collective_id=0, has_side_effects=True, vmem_limit_bytes=60 * 1024 * 1024
        ),
    )(image_owner.T, anchor[None, :], loader_shard.T, images, ids, sentences)
    if block != cap:
        meta = meta.reshape(n, SUB, LANES)[:, 0, cap + 1]
        picked = got_txt.reshape(n, block, feature)[jnp.maximum(meta - 1, 0), :cap]
        text = jnp.where((meta > 0)[:, None, None], picked, jnp.zeros_like(picked))
        image = got_img.reshape(n, block, feature)[:, :cap]
        return (image.reshape(n * cap, feature), text.reshape(n * cap, feature))
    return pl.pallas_call(
        functools.partial(place_kernel, n, block, cap + 1),
        out_shape=(half, half),
        in_specs=[pl.BlockSpec(memory_space=pltpu.SMEM), vmem, vmem],
        out_specs=(anywhere, anywhere),
        scratch_shapes=[slots, dma((1 + n,))],
    )(meta, got_img, got_txt)


def solution(mesh):
    return jax.shard_map(
        shards,
        mesh=mesh,
        in_specs=(
            P(("groups", "docs"), None),
            P("groups"),
            P(("groups", "docs"), None),
            P(("groups", "docs"), None),
            P(("groups", "docs")),
            P(("groups", "docs"), None),
        ),
        out_specs=(P(("groups", "docs"), None), P(("groups", "docs"), None)),
        check_vma=False,
    )
```

profile of v0, /device:TPU:0, one launch (start us, length us, event | category | flops | bytes accessed | tf_op | source)
XLA Modules:
  0.0 99.4 jit_solution(11247734148503213141)
XLA Ops:
  0.6 0.8 pad_dynamic-slice_fusion
  1.4 0.6 broadcast_in_dim.7.ids_ref
  2.0 94.0 %shard_map.77 = (bf16[512,1280]{1,0:T(8,128)(2,1)}, bf16[512,1280]{1,0:T(8,128)(2,1)}, s32[128,128]{1,0:T(8,128)}) custom-call(s32[1,256]{1,0:T(1,128)} %bitcast.3, s32[1,256]{1,0:T(1,128)} %bitcast.4, s32[1,256]{1,0:T(1,128)} %bitcast.5, bf16[256,1280]{1,0:T(8,128)(2,1)} %images_ref.1, s32[1,2112]{1,0:T(1,128)} %broadcast_in_dim.7.ids_ref, ...), custom_call_target="tpu_custom_call" | custom-call | tf_op jit(solution)/shard_map/pallas_call | solution.py:279
  96.0 3.4 %shard_map.78 = (bf16[512,1280]{1,0:T(8,128)(2,1)}, bf16[512,1280]{1,0:T(8,128)(2,1)}) custom-call(s32[128,128]{1,0:T(8,128)} %get-tuple-element.5.meta_ref, bf16[512,1280]{1,0:T(8,128)(2,1)} %get-tuple-element.6.img_ref, bf16[512,1280]{1,0:T(8,128)(2,1)} %get-tuple-element.7.txt_ref), custom_call_target="tpu_custom_call" | custom-call | tf_op jit(solution)/shard_map/pallas_call | solution.py:304
where the time goes:
time: 101 us; the launch traced here: 99.4 us
  Pallas kernels  97.3 us (96%)
  local copies, waits for them, and re-layouts  1.41 us (1%)
    pallas_call x1, Pallas kernels, shards(): pl.pallas_call(functools.partial(exchange_kernel, n, cap, block, tile), o...  94 us
    pallas_call x1, Pallas kernels, shards(): pl.pallas_call(functools.partial(place_kernel, n, block, cap + 1), out_sh...  3.36 us

commit v1 on v0

v1 whole, which is shorter than its diff:
```python
import functools

import jax
import jax.numpy as jnp
from jax import lax
from jax.experimental import pallas as pl
from jax.experimental.pallas import tpu as pltpu
from jax.sharding import PartitionSpec as P

MOST_SENT = 32
LANES = 128
SUB = 8
MESH = pl.DeviceIdType.MESH
HIGH = lax.Precision.HIGHEST
TRANS_LHS = (((0,), (0,)), ((), ()))
TRANS_RHS = (((1,), (1,)), ((), ()))


def iota(shape, dim):
    return lax.broadcasted_iota(jnp.int32, shape, dim)


def earlier(keys, n, above):
    onehot = (keys == iota((n, keys.shape[1]), 0)).astype(jnp.float32)
    counts = jnp.dot(onehot.astype(jnp.bfloat16), above, preferred_element_type=jnp.float32)
    return onehot, counts


def cuts(n, count, chunks):
    return [min(count, n * SUB * (q + 1)) for q in range(chunks - 1)] + [count]


def exchange_kernel(
    n, cap, chunks, owner_hbm, anchor_hbm, shard_hbm, images_hbm, ids_hbm, sent_hbm,
    img_out, txt_out,
    ext, owner_ref, anchor_ref, shard_ref, images_ref, own_ids, prev_ids, next_ids,
    ordered, keys_ref, far_images, far_keys, disp, shrd, far_disp, far_shrd,
    arrived, far_arrived, aligned, tsend, txt_in, meta_s, meta_in, target_ref,
    load_sem, local_sem, halo_send, halo_recv, raw_send, raw_recv, send_sem, recv_sem,
):
    me = lax.axis_index("docs")
    half = n // 2
    first = lax.div(me, half) * half
    across = lax.rem(first + half, n)
    partner = lax.rem(me + half, n)
    own_rows, feature = sent_hbm.shape
    width = ext.shape[0]
    count = images_hbm.shape[0]
    block = chunks * SUB
    group = half * SUB
    stripe = n * SUB
    part = half * block
    id_rows = own_rows // LANES
    temper = feature ** (-0.5)

    barrier = pltpu.get_barrier_semaphore()

    @pl.loop(1, n)
    def _(k):
        pl.semaphore_signal(barrier, inc=1, device_id={"docs": lax.rem(me + k, n)}, device_id_type=MESH)

    before = pl.multiple_of(jnp.maximum(me * id_rows - SUB, 0), SUB)
    after = pl.multiple_of(jnp.minimum(me * id_rows + id_rows, n * id_rows - SUB), SUB)
    loads = [
        pltpu.make_async_copy(src, dst, load_sem.at[i])
        for i, (src, dst) in enumerate((
            (owner_hbm, owner_ref),
            (anchor_hbm, anchor_ref),
            (shard_hbm, shard_ref),
            (images_hbm, images_ref),
            (ids_hbm.at[pl.ds(pl.multiple_of(me * id_rows, SUB), id_rows)], own_ids),
            (ids_hbm.at[pl.ds(before, SUB)], prev_ids),
            (ids_hbm.at[pl.ds(after, SUB)], next_ids),
            (sent_hbm, ext.at[pl.ds(0, own_rows)]),
        ))
    ]
    for copy in loads:
        copy.start()

    gap = LANES - 2 * MOST_SENT
    ext[pl.ds(own_rows + MOST_SENT, gap), :] = jnp.zeros((gap, feature), ext.dtype)
    above = (iota((count, count), 0) < iota((count, count), 1)).astype(jnp.bfloat16)
    for copy in loads[:3]:
        copy.wait()
    owner, anchor, shard = owner_ref[...], anchor_ref[...], shard_ref[...]
    onehot, counts = earlier(owner, n, above)
    rank = jnp.sum(counts * onehot, axis=0, keepdims=True).astype(jnp.int32)

    levels = -(-cap // SUB) * SUB
    onehot, counts = earlier(rank, levels, above)
    lower = (iota((levels, levels), 1) < iota((levels, levels), 0)).astype(jnp.bfloat16)
    under = jnp.dot(lower, onehot.astype(jnp.bfloat16), preferred_element_type=jnp.float32)
    under = jnp.sum(under, axis=1, keepdims=True)
    order = jnp.sum((counts + under) * onehot, axis=0, keepdims=True).astype(jnp.int32)
    sorter = (iota((count, count), 0) == order).astype(jnp.bfloat16)
    row = iota((SUB, count), 0)
    facts = jnp.where(row == 0, owner, jnp.where(row == 1, rank, shard))
    keys_ref[...] = lax.dot_general(
        facts.astype(jnp.bfloat16), sorter, TRANS_RHS, preferred_element_type=jnp.float32
    ).astype(jnp.int32)

    lane = iota((LANES, count), 0)
    lead = rank == 0
    for_owner = jnp.where(lane == rank, anchor + 1, 0) + jnp.where((lane == cap) & lead, shard + 1, 0)
    for_shard = jnp.where((lane == cap + 1) & lead, owner + 1, 0)
    keyed = lax.div(iota((stripe, count), 0), SUB)
    meta = lax.dot_general(
        (keyed == owner).astype(jnp.float32), for_owner.astype(jnp.float32), TRANS_RHS,
        precision=HIGH, preferred_element_type=jnp.float32,
    ) + lax.dot_general(
        (keyed == shard).astype(jnp.float32), for_shard.astype(jnp.float32), TRANS_RHS,
        precision=HIGH, preferred_element_type=jnp.float32,
    )
    meta_s[...] = meta.astype(jnp.int32)
    loads[3].wait()

    def pick(ref, start, size, place, values):
        tile = min(256, size)

        @pl.loop(0, size // tile)
        def _(t):
            base = pl.multiple_of(t * tile, tile)
            table = (place == iota((tile, place.shape[1]), 0) + base).astype(jnp.bfloat16)
            ref[pl.ds(start + base, tile), :] = jnp.dot(
                table, values, preferred_element_type=jnp.float32
            ).astype(jnp.bfloat16)

    def to_owner(who, order, q):
        inside = (who >= first) & (who < first + half)
        spot = (who - first) * SUB + lax.rem(order, SUB)
        if q is None:
            return jnp.where(inside, lax.div(order, SUB) * group + spot, -1)
        return jnp.where(inside & (lax.div(order, SUB) == q), spot, -1)

    pick(ordered, 0, count, order, images_ref[...])
    pick(disp, 0, part, to_owner(owner, rank, None), images_ref[...])
    pick(shrd, 0, part, (shard - first) * block + rank, images_ref[...])

    edges = cuts(n, count, chunks)
    ends = sorted(set(edges))

    def raw(piece):
        if piece < len(ends):
            low = ends[piece - 1] if piece else 0
            rows = pl.ds(low, ends[piece] - low)
            src, dst = ordered.at[rows], far_images.at[rows]
        else:
            src, dst = keys_ref, far_keys
        return pltpu.make_async_remote_copy(
            src_ref=src, dst_ref=dst, send_sem=raw_send.at[piece], recv_sem=raw_recv.at[piece],
            device_id={"docs": partner}, device_id_type=MESH,
        )

    def halo(way):
        to = lax.rem(me + 1, n) if way == 0 else lax.rem(me + n - 1, n)
        src = own_rows - MOST_SENT if way == 0 else 0
        dst = own_rows + LANES - MOST_SENT if way == 0 else own_rows
        return pltpu.make_async_remote_copy(
            src_ref=sent_hbm.at[pl.ds(src, MOST_SENT)], dst_ref=ext.at[pl.ds(dst, MOST_SENT)],
            send_sem=halo_send.at[way], recv_sem=halo_recv.at[way],
            device_id={"docs": to}, device_id_type=MESH,
        )

    META, SHRD, FSHRD, DISP = 0, 1, 2, 3
    FDISP, TEXT = DISP + chunks, DISP + 2 * chunks

    def route_of(kind, peer, sender):
        if kind == META:
            return meta_s, peer * SUB, meta_in, sender * SUB, SUB
        if kind == SHRD:
            return shrd, (peer - first) * block, img_out, sender * block, block
        if kind == FSHRD:
            return far_shrd, (peer - first) * block, img_out, lax.rem(sender + half, n) * block, block
        if kind < FDISP:
            base = (kind - DISP) * group
            return disp, base + (peer - first) * SUB, arrived, base + (sender - first) * SUB, SUB
        if kind < TEXT:
            base = (kind - FDISP) * group
            return far_disp, base + (peer - first) * SUB, far_arrived, base + (sender - first) * SUB, SUB
        base = (kind - TEXT) * stripe
        return tsend, base + peer * SUB, txt_in, base + sender * SUB, SUB

    def views(kind, peer, sender):
        src, src_at, dst, dst_at, size = route_of(kind, peer, sender)
        return (
            src.at[pl.ds(pl.multiple_of(src_at, size), size)],
            dst.at[pl.ds(pl.multiple_of(dst_at, size), size)],
        )

    def remote(kind, peer, sender):
        src, dst = views(kind, peer, sender)
        return pltpu.make_async_remote_copy(
            src_ref=src, dst_ref=dst,
            send_sem=send_sem.at[kind, peer], recv_sem=recv_sem.at[kind, sender],
            device_id={"docs": peer}, device_id_type=MESH,
        )

    def local(kind):
        src, dst = views(kind, me, me)
        return pltpu.make_async_copy(src, dst, local_sem.at[kind])

    def each(kind, act):
        if kind == META or kind >= TEXT:

            @pl.loop(0, half)
            def _(k):
                act(across + lax.rem(me - first + k, half))

        @pl.loop(1, half)
        def _(k):
            act(first + lax.rem(me - first + k, half))

    def start(kind):
        each(kind, lambda peer: remote(kind, peer, me).start())
        local(kind).start()

    def sent(kind):
        each(kind, lambda peer: remote(kind, peer, me).wait_send())

    def landed(kind):
        each(kind, lambda peer: remote(kind, peer, peer).wait_recv())
        local(kind).wait()

    pl.semaphore_wait(barrier, n - 1)
    start(META)
    halo(0).start()
    halo(1).start()
    raw(len(ends)).start()
    for q in range(chunks):
        start(DISP + q)
    start(SHRD)
    for piece in range(len(ends)):
        raw(piece).start()

    for copy in loads[4:]:
        copy.wait()
    for way in (0, 1):
        halo(way).wait_recv()
    landed(META)
    line = iota((1, LANES), 1)
    tail = jnp.where((line < MOST_SENT) & (me < n - 1), next_ids[0:1, :], -1)
    tail = jnp.where((line >= LANES - MOST_SENT) & (me > 0), prev_ids[SUB - 1 : SUB, :], tail)
    ids = jnp.concatenate([own_ids[r : r + 1, :] for r in range(id_rows)] + [tail], axis=1)

    def align(rows_ref, base, size, head):
        begin = pl.multiple_of(head * SUB, SUB)
        if size >= group:
            picked = jnp.concatenate([meta_in[pl.ds(begin, group), :]] * (size // group), axis=0)
        else:
            picked = meta_in[pl.ds(begin + base % group, size), :]
        spot = iota((size, 1), 0) + base
        inner = lax.rem(spot, SUB)
        step = lax.div(spot, group) * SUB + inner
        lanes = iota((size, LANES), 1)
        anchored = jnp.sum(jnp.where((lanes == step) & (lanes < cap), picked, 0), axis=1, keepdims=True)
        goal = jnp.sum(jnp.where(lanes == cap, picked, 0), axis=1, keepdims=True)
        target = (goal - 1) * SUB + inner
        filled = anchored > 0
        here = iota((size, width), 1) == anchored - 1
        doc = jnp.sum(jnp.where(here, ids, 0), axis=1, keepdims=True)
        doc = jnp.where(filled, doc, -2)
        scores = lax.dot_general(
            rows_ref[pl.ds(base, size), :], ext[...], TRANS_RHS, preferred_element_type=jnp.float32
        ) * temper
        member = doc == ids
        peak = jnp.max(jnp.where(member, scores, -1e30), axis=1, keepdims=True)
        raised = jnp.where(member, jnp.exp(scores - peak), 0.0)
        total = jnp.sum(raised, axis=1, keepdims=True)
        weights = (raised / jnp.where(filled, total, 1.0)).astype(jnp.bfloat16)
        result = jnp.dot(weights, ext[...], preferred_element_type=jnp.float32).astype(jnp.bfloat16)
        extra = 0 if rows_ref is arrived else group
        for low in range(0, size, group):
            at = (base + low) // group * stripe + (base + low) % group + extra
            high = min(size, low + group)
            aligned[pl.ds(at, high - low), :] = result[low:high]
            target_ref[pl.ds(at, high - low), :] = target[low:high]

    def align_all(rows_ref, base, rows, head):
        tile = min(256, rows)
        for low in range(base, base + rows, tile):
            align(rows_ref, low, tile, head)

    def route(q):
        begin = q * stripe
        tile = min(256, stripe)
        for base in range(0, stripe, tile):
            table = target_ref[pl.ds(begin, stripe), :] == iota((stripe, tile), 1) + base
            tsend[pl.ds(begin + base, tile), :] = lax.dot_general(
                table.astype(jnp.bfloat16), aligned[pl.ds(begin, stripe), :], TRANS_LHS,
                preferred_element_type=jnp.float32,
            ).astype(jnp.bfloat16)

    def place(q):
        wanted = jnp.sum(
            jnp.where(iota((stripe, LANES), 1) == cap + 1, meta_in[...], 0), axis=1, keepdims=True
        )
        wanted = (wanted - 1) * SUB + lax.rem(iota((stripe, 1), 0), SUB)
        tile = min(256, stripe)
        for base in range(0, stripe, tile):
            table = wanted[base : base + tile] == iota((tile, stripe), 1)
            moved = jnp.dot(
                table.astype(jnp.bfloat16), txt_in[pl.ds(q * stripe, stripe), :],
                preferred_element_type=jnp.float32,
            ).astype(jnp.bfloat16)
            for low in range(0, tile, SUB):
                at = (base + low) // SUB * block + q * SUB
                txt_out[pl.ds(at, SUB), :] = moved[low : low + SUB]

    for q in range(chunks):
        landed(DISP + q)
    align_all(arrived, 0, part, first)

    raw(len(ends)).wait_recv()
    far_owner, far_rank, far_shard = far_keys[0:1, :], far_keys[1:2, :], far_keys[2:3, :]

    def far_fill(q):
        rows = edges[q]
        place_of = to_owner(far_owner, far_rank, q)[:, :rows]
        pick(far_disp, q * group, group, place_of, far_images[pl.ds(0, rows), :])
        start(FDISP + q)

    ready = []
    for piece, end in enumerate(ends):
        last = piece == len(ends) - 1
        raw(piece).wait_recv()
        due = [q for q in range(chunks) if edges[q] == end]
        for i, q in enumerate(due):
            far_fill(q)
            if last and i == 0:
                for old in ready:
                    start(TEXT + old)
        if last:
            pick(far_shrd, 0, part, (far_shard - first) * block + far_rank, far_images[...])
            start(FSHRD)
        for q in due:
            landed(FDISP + q)
            align_all(far_arrived, q * group, group, across)
            route(q)
            if last:
                start(TEXT + q)
            else:
                ready.append(q)

    landed(SHRD)
    landed(FSHRD)
    for q in range(chunks):
        landed(TEXT + q)
        place(q)
    for way in (0, 1):
        halo(way).wait_send()
    for piece in range(len(ends) + 1):
        raw(piece).wait_send()
    for kind in range(TEXT + chunks):
        sent(kind)


def store_kernel(img_ref, txt_ref, img_out, txt_out, sems):
    copies = [
        pltpu.make_async_copy(src, dst, sems.at[i])
        for i, (src, dst) in enumerate(((img_ref, img_out), (txt_ref, txt_out)))
    ]
    for copy in copies:
        copy.start()
    for copy in copies:
        copy.wait()


def shards(sentences, sent_doc, images, image_owner, anchor, loader_shard):
    n = lax.axis_size("docs")
    own_rows, feature = sentences.shape
    count = images.shape[0]
    cap = max(4, 2 * count // n)
    chunks = -(-cap // SUB)
    block = chunks * SUB
    rows = n * block
    width = own_rows + LANES
    pieces = len(set(cuts(n, count, chunks)))
    kinds = 3 + 3 * chunks
    slots = pltpu.VMEM((rows, feature), jnp.bfloat16)
    some = pltpu.VMEM((rows // 2, feature), jnp.bfloat16)
    held = pltpu.VMEM((count, feature), jnp.bfloat16)
    vector = pltpu.VMEM((1, count), jnp.int32)
    table = pltpu.VMEM((n * SUB, LANES), jnp.int32)
    anywhere = pl.BlockSpec(memory_space=pl.ANY)
    dma = pltpu.SemaphoreType.DMA
    vmem = pl.BlockSpec(memory_space=pltpu.VMEM)
    image, text = pl.pallas_call(
        functools.partial(exchange_kernel, n, cap, chunks),
        out_shape=(slots, slots),
        in_specs=[anywhere] * 6,
        out_specs=(vmem, vmem),
        scratch_shapes=[
            pltpu.VMEM((width, feature), jnp.bfloat16),
            vector, vector, vector, held,
            pltpu.VMEM((own_rows // LANES, LANES), jnp.int32),
            pltpu.VMEM((SUB, LANES), jnp.int32),
            pltpu.VMEM((SUB, LANES), jnp.int32),
            held, pltpu.VMEM((SUB, count), jnp.int32),
            held, pltpu.VMEM((SUB, count), jnp.int32),
            some, some, some, some, some, some, slots, slots, slots, table, table,
            pltpu.VMEM((rows, 1), jnp.int32),
            dma((8,)), dma((kinds,)), dma((2,)), dma((2,)), dma((pieces + 1,)), dma((pieces + 1,)),
            dma((kinds, n)), dma((kinds, n)),
        ],
        compiler_params=pltpu.CompilerParams(
            collective_id=0, has_side_effects=True, vmem_limit_bytes=48 * 1024 * 1024
        ),
    )(image_owner.T, anchor[None, :], loader_shard.T, images, sent_doc.reshape(-1, LANES), sentences)
    if block != cap:
        return tuple(
            array.reshape(n, block, feature)[:, :cap].reshape(n * cap, feature) for array in (image, text)
        )
    image, text = (pltpu.with_memory_space_constraint(array, pltpu.VMEM) for array in (image, text))
    full = jax.ShapeDtypeStruct((rows, feature), jnp.bfloat16)
    return pl.pallas_call(
        store_kernel,
        out_shape=(full, full),
        in_specs=[vmem, vmem],
        out_specs=(anywhere, anywhere),
        scratch_shapes=[dma((2,))],
    )(image, text)


def solution(mesh):
    return jax.shard_map(
        shards,
        mesh=mesh,
        in_specs=(
            P(("groups", "docs"), None),
            P("groups"),
            P(("groups", "docs"), None),
            P(("groups", "docs"), None),
            P(("groups", "docs")),
            P(("groups", "docs"), None),
        ),
        out_specs=(P(("groups", "docs"), None), P(("groups", "docs"), None)),
        check_vma=False,
    )
```

time: 101 us -> 91.7 us (0.908); the launches traced: 99.4 us -> 91.5 us
  Pallas kernels: 97.3 us -> 86.7 us
  local copies, waits for them, and re-layouts: 1.41 us -> 4.02 us
    pallas_call x2, Pallas kernels: 97.3 us -> 86.7 us  [the longest x1 85.2 us: shards(): pl.pallas_call(functools.partial(exchange_kernel, n, cap, chunks), out_sh...]
    unnamed x0 -> x10, local copies, waits for them, and re-layouts: none -> 4.02 us
where the time goes in v1:
time: 91.7 us; the launch traced here: 91.5 us
  Pallas kernels  86.7 us (95%)
  local copies, waits for them, and re-layouts  4.02 us (4%)
    pallas_call x1, Pallas kernels, shards(): pl.pallas_call(functools.partial(exchange_kernel, n, cap, chunks), out_sh...  85.2 us
    unnamed x10, local copies, waits for them, and re-layouts  4.02 us

profile of v1, /device:TPU:0, one launch (start us, length us, event | category | flops | bytes accessed | tf_op | source)
XLA Modules:
  0.0 91.5 jit_solution(6273562495616456005)
XLA Ops:
  0.6 0.0 copy-start
  0.6 1.1 %copy-done = bf16[256,1280]{1,0:T(8,128)(2,1)S(1)} copy-done((bf16[256,1280]{1,0:T(8,128)(2,1)S(1)}, bf16[256,1280]{1,0:T(8,128)(2,1)}, u32[]{:S(2)}) %copy-start) | copy-done | bytes 655384
  1.7 0.0 copy-start.1
  1.7 0.9 copy-done.1
  2.6 0.0 copy-start.2
  2.6 0.7 copy-done.2
  3.3 0.0 copy-start.3
  3.3 0.7 copy-done.3
  4.0 0.0 copy-start.4
  4.0 0.7 copy-done.4
  4.7 85.2 %shard_map.77 = (bf16[512,1280]{1,0:T(8,128)(2,1)S(1)}, bf16[512,1280]{1,0:T(8,128)(2,1)S(1)}) custom-call(s32[1,256]{1,0:T(1,128)S(1)} %bitcast.5, s32[1,256]{1,0:T(1,128)S(1)} %bitcast.6, s32[1,256]{1,0:T(1,128)S(1)} %bitcast.7, bf16[256,1280]{1,0:T(8,128)(2,1)S(1)} %copy-done, s32[256,128]{1,0:T(8,128)S(1)} %bitcast.4, bf16[2048,1280]{1,0:T(8,128)(2,1)} %sent_hbm.1), custom_call_target="tpu_custom_call" | custom-call | tf_op jit(solution)/shard_map/pallas_call | solution.py:387
  89.8 1.5 %shard_map.78 = (bf16[512,1280]{1,0:T(8,128)(2,1)}, bf16[512,1280]{1,0:T(8,128)(2,1)}) custom-call(bf16[512,1280]{1,0:T(8,128)(2,1)S(1)} %get-tuple-element.4.img_ref, bf16[512,1280]{1,0:T(8,128)(2,1)S(1)} %get-tuple-element.5.txt_ref), custom_call_target="tpu_custom_call" | custom-call | tf_op jit(solution)/shard_map/pallas_call | solution.py:415
Async XLA Ops:
  0.6 1.1 %copy-start = (bf16[256,1280]{1,0:T(8,128)(2,1)S(1)}, bf16[256,1280]{1,0:T(8,128)(2,1)}, u32[]{:S(2)}) copy-start(bf16[256,1280]{1,0:T(8,128)(2,1)} %images_hbm.1) | copy-start | bytes 1966084
  1.7 0.9 copy-start.1
  2.6 0.7 copy-start.2
  3.3 0.7 copy-start.3
  4.0 0.7 copy-start.4
